TPU v7x, 32 devices: a whole 2x2x4 slice. The times are simulated.
32 devices in a mesh: iface: 8 (over z, y), dom: 4 (over x, core).
Axes of the slice: x: 2, y: 2, z: 4, core: 2. Of those that a mesh axis runs over, the one named last changes fastest.
Arguments:
- interface: float32 [131072], P(('iface', 'dom')), may hold values from -6 to 6
- previous_residual: float32 [131072], P(('iface', 'dom')), may hold values from -6 to 6
- previous_estimate: float32 [131072], P(('iface', 'dom')), may hold values from -6 to 6
- forcing: float32 [131072], P(('iface', 'dom')), may hold values from -60 to 60
- stiffness: float32 [131072], P(('iface', 'dom')), may hold values from 0.2 to 0.6
- history_residual: float32 [100, 131072], P(None, ('iface', 'dom')), may hold values from -40 to 40
- history_estimate: float32 [100, 131072], P(None, ('iface', 'dom')), may hold values from -6 to 6
Outputs:
- interface_next: float32 [131072], P(('iface', 'dom'))
- residual_last: float32 [131072], P(('iface', 'dom'))
All inputs are finite; a program needn't handle non-finite values.
Results may differ from a plain program's by a relative error of at most 0.0003.
Values sent between devices are 32-bit elements; how exact they have to be, the bound alone decides.
A program may use at most 64 MiB of HBM per device.

v0:
```python
import functools
import jax
import jax.numpy as jnp
from jax import lax
from jax.experimental import pallas as pl
from jax.experimental.pallas import tpu as pltpu
from jax.sharding import PartitionSpec as P

ITERS = 3
coupling = 0.25
LANES = 128
AXES = ("iface", "dom")
F32 = jnp.float32


def invert(matrix, rows):
    lane8 = lax.broadcasted_iota(jnp.int32, (8, LANES), 1)
    sub8 = lax.broadcasted_iota(jnp.int32, (8, LANES), 0)
    blocks = [matrix[8 * at : 8 * at + 8, :] for at in range(rows // 8)]
    for step in range(rows // 8):
        first = 8 * step
        inside = (lane8 >= first) & (lane8 < first + 8)
        unit = (lane8 - first == sub8).astype(F32)
        pivots = blocks[step]
        columns = [jnp.broadcast_to(pivots[:, first + at : first + at + 1], (8, LANES)) for at in range(8)]
        panel = jnp.where(inside, unit, pivots)
        for at in range(8):
            inverse = 1.0 / columns[at][at : at + 1, :]
            own = sub8 == at
            factor = columns[at]
            row = panel[at : at + 1, :] * inverse
            panel = jnp.where(own, row, panel - factor * row)
            for later in range(at + 1, 8):
                row = columns[later][at : at + 1, :] * inverse
                columns[later] = jnp.where(own, row, columns[later] - factor * row)
        for other in range(rows // 8):
            if other != step:
                block = blocks[other]
                total = jnp.where(inside, 0.0, block)
                for at in range(8):
                    column = jnp.broadcast_to(block[:, first + at : first + at + 1], (8, LANES))
                    total = total - column * panel[at : at + 1, :]
                blocks[other] = total
        blocks[step] = panel
    return jnp.concatenate(blocks, axis=0)


def kernel(
    sizes,
    interface,
    previous_residual,
    previous_estimate,
    forcing,
    stiffness,
    history_residual,
    history_estimate,
    next_ref,
    last_ref,
    cur_x,
    est_x,
    force_x,
    stiff_x,
    old_res,
    hist_v,
    hist_w,
    new_v,
    new_w,
    dots_in,
    square,
    part_out,
    part_in,
    mid_in,
    gathered,
    row_in,
    piece_sem,
    load_sem,
    halo_sem,
    wide_sem,
    part_sem,
    mid_sem,
    gather_sem,
    row_sem,
):
    n_iface, n_dom, hist, base, rows, width, share, depth = sizes
    count = n_iface * n_dom
    at_iface, at_dom = lax.axis_index("iface"), lax.axis_index("dom")
    me = at_iface * n_dom + at_dom
    last = count - 1
    full = width + 2 * LANES
    ifaces = [lax.rem(at_iface + step, n_iface) for step in range(n_iface)]
    doms = [lax.rem(at_dom + step, n_dom) for step in range(n_dom)]
    everyone = [(a, b) for a in ifaces for b in doms][1:]

    def place(index):
        return (index // n_dom, lax.rem(index, n_dom))

    barrier = pltpu.get_barrier_semaphore()

    def greet(device):
        pl.semaphore_signal(barrier, inc=1, device_id=device, device_id_type=pl.DeviceIdType.MESH)

    for iface in ifaces[1:]:
        greet((iface, at_dom))
    right = place(lax.rem(me + 1, count))
    left = place(lax.rem(me + last, count))
    greet(right)
    greet(left)
    for dom in doms[1:]:
        greet((at_iface, dom))

    own = pl.ds(LANES, width)

    def piece(at):
        span = pl.ds(pl.multiple_of(at * depth, depth), depth)
        return pltpu.make_async_copy(history_residual.at[:, span], hist_v.at[:, span], piece_sem.at[at])

    for at in range(width // depth):
        piece(at).start()
    small = []
    for at, (source, target) in enumerate(
        [
            (interface, cur_x.at[:, own]),
            (previous_estimate, est_x.at[:, own]),
            (forcing, force_x.at[:, own]),
            (stiffness, stiff_x.at[:, own]),
            (previous_residual, old_res),
        ]
    ):
        copy = pltpu.make_async_copy(source, target, load_sem.at[1 + at])
        copy.start()
        small.append(copy)
    load_w = pltpu.make_async_copy(history_estimate, hist_w.at[:, own], load_sem.at[0])
    new_v[...] = jnp.zeros(new_v.shape, F32)
    new_w[...] = jnp.zeros(new_w.shape, F32)

    def add_gram(at, total):
        piece(at).wait()
        block = hist_v[:, pl.ds(pl.multiple_of(at * depth, depth), depth)]
        one = block.astype(jnp.bfloat16)
        rest = block - one.astype(F32)
        two = rest.astype(jnp.bfloat16)
        three = (rest - two.astype(F32)).astype(jnp.bfloat16)
        main = jnp.concatenate([one, two], axis=1)
        side = jnp.concatenate([two, three], axis=1), jnp.concatenate([one, one], axis=1)
        dims = (((1,), (1,)), ((), ()))
        return (
            total[0] + lax.dot_general(main, main, dims, preferred_element_type=F32),
            total[1] + lax.dot_general(*side, dims, preferred_element_type=F32),
        )

    empty = jnp.zeros((hist, hist), F32)
    main, side = lax.fori_loop(0, width // depth, add_gram, (empty, empty))
    load_w.start()
    square[...] = jnp.zeros(square.shape, F32)
    square[0:hist, 0:hist] = side
    mirrored = square[...].T
    square[0:hist, 0:hist] = main + side
    square[...] = square[...] + mirrored
    lane8 = lax.broadcasted_iota(jnp.int32, (8, LANES), 1)
    blocks = (base // 8 + 1) // 2 * 2
    pairs = blocks // 2

    def natural(block):
        return (lane8 >= 8 * block) & (lane8 < 8 * blocks)

    for pair in range(n_dom * share):
        where = (pair // share, pl.ds(8 * (pair % share), 8), slice(None))
        if pair < pairs:
            other = blocks - 1 - pair
            moved = pltpu.roll(square[8 * other : 8 * other + 8, :], 8 * pair + 8, 1)
            part_out[where] = jnp.where(natural(pair), square[8 * pair : 8 * pair + 8, :], moved)
        else:
            part_out[where] = jnp.zeros((8, LANES), F32)
    part_in[at_dom] = part_out[at_dom]
    for copy in small:
        copy.wait()
    pl.semaphore_wait(barrier, n_iface + n_dom)

    def edges(refs, sems):
        copies = []
        for at, ref in enumerate(refs):
            for side, (source, target, device) in enumerate([(width, 0, right), (LANES, width + LANES, left)]):
                copies.append(
                    pltpu.make_async_remote_copy(
                        src_ref=ref.at[:, pl.ds(source, LANES)],
                        dst_ref=ref.at[:, pl.ds(target, LANES)],
                        send_sem=sems.at[0, at, side],
                        recv_sem=sems.at[1, at, side],
                        device_id=device,
                        device_id_type=pl.DeviceIdType.MESH,
                    )
                )
        return copies[0::2], copies[1::2]

    def edges_start(copies):
        for side, some in enumerate([me < last, me > 0]):

            @pl.when(some)
            def _():
                for copy in copies[side]:
                    copy.start()

    def edges_wait(copies):
        for side, (sent, received) in enumerate([(me < last, me > 0), (me > 0, me < last)]):

            @pl.when(sent)
            def _():
                for copy in copies[side]:
                    copy.wait_send()

            @pl.when(received)
            def _():
                for copy in copies[side]:
                    copy.wait_recv()

    def send(source, target, sems, device):
        pltpu.make_async_remote_copy(
            src_ref=source,
            dst_ref=target,
            send_sem=sems.at[0],
            recv_sem=sems.at[1],
            device_id=device,
            device_id_type=pl.DeviceIdType.MESH,
        ).start()

    def arrive(target, many, sems):
        most = target.at[pl.ds(0, many)]
        pltpu.make_async_copy(most, most, sems.at[1]).wait()
        pltpu.make_async_copy(most, most, sems.at[0]).wait()

    for dom in doms[1:]:
        send(part_out.at[dom], part_in.at[at_dom], part_sem, (at_iface, dom))
    halos = edges([cur_x, est_x, force_x, stiff_x], halo_sem)
    edges_start(halos)
    wide = edges([hist_w], wide_sem)

    lane = lax.broadcasted_iota(jnp.int32, (1, full), 1)
    outside = ((me == 0) & (lane < LANES)) | ((me == count - 1) & (lane >= LANES + width))
    eye = (
        lax.broadcasted_iota(jnp.int32, (rows, LANES), 0) == lax.broadcasted_iota(jnp.int32, (rows, LANES), 1)
    ).astype(F32)
    row_at = lax.broadcasted_iota(jnp.int32, (rows, LANES), 0)
    ones = jnp.ones((8, LANES), F32)

    def column_of(row):
        return jnp.broadcast_to(jnp.sum(eye * row, axis=1, keepdims=True), (rows, LANES))

    def over_rows(value):
        return jnp.sum(value, axis=0, keepdims=True)

    def begin(iteration):
        current = cur_x[...]
        before = pltpu.roll(current, 1, 1)
        after = pltpu.roll(current, full - 1, 1)
        estimate = force_x[...] + stiff_x[...] * jnp.tanh(current) + coupling * (before + after)
        residual = (estimate - current)[:, LANES : LANES + width]
        new_w[iteration : iteration + 1, :] = estimate - est_x[...]
        est_x[...] = estimate
        new_v[iteration : iteration + 1, :] = residual - old_res[...]
        old_res[...] = residual

        def add(at, totals):
            span = pl.ds(pl.multiple_of(at * LANES, LANES), LANES)
            block, extra = hist_v[:, span], new_v[:, span]
            res, new = old_res[:, span], new_v[iteration : iteration + 1, span]
            return (totals[0] + block * res, totals[1] + block * new, totals[2] + extra * res, totals[3] + extra * new)

        zero, few = jnp.zeros((hist, LANES), F32), jnp.zeros((8, LANES), F32)
        totals = lax.fori_loop(0, width // LANES, add, (zero, zero, few, few), unroll=4)
        dots_in[iteration] = jnp.zeros((2, LANES), F32)
        for which in range(4):
            sums = lax.dot_general(
                ones, totals[which], (((1,), (1,)), ((), ())), precision=lax.Precision.HIGHEST, preferred_element_type=F32
            )
            if which < 2:
                dots_in[iteration, which : which + 1, 0:hist] = sums[0:1, :]
            else:
                dots_in[iteration, which - 2 : which - 1, base : base + 8] = sums[0:1, :]
        row_in[iteration, me] = dots_in[iteration]
        for device in everyone:
            send(dots_in.at[iteration], row_in.at[iteration, me], row_sem.at[iteration], device)

    def sums_of(iteration):
        arrive(row_in.at[iteration], last, row_sem.at[iteration])
        return jnp.sum(row_in[iteration], axis=0)

    arrive(part_in, n_dom - 1, part_sem)
    mid_in[at_iface] = jnp.sum(part_in[...], axis=0)
    for iface in ifaces[1:]:
        send(mid_in.at[at_iface], mid_in.at[at_iface], mid_sem, (iface, at_dom))
    edges_wait(halos)
    cur_x[...] = jnp.where(outside, 0.0, cur_x[...])
    begin(0)
    load_w.wait()
    arrive(mid_in, n_iface - 1, mid_sem)
    gathered[at_dom] = jnp.sum(mid_in[...], axis=0)
    for dom in doms[1:]:
        send(gathered.at[at_dom], gathered.at[at_dom], gather_sem, (at_iface, dom))
    edges_start(wide)
    arrive(gathered, n_dom - 1, gather_sem)
    for pair in range(pairs):
        other = blocks - 1 - pair
        packed = gathered[pair // share, pl.ds(8 * (pair % share), 8), :]
        square[8 * pair : 8 * pair + 8, :] = jnp.where(natural(pair), packed, 0.0)
        moved = pltpu.roll(packed, LANES - 8 * pair - 8, 1)
        square[8 * other : 8 * other + 8, :] = jnp.where(natural(other), moved, 0.0)
    upper = square[...]
    lane_block = lax.broadcasted_iota(jnp.int32, (LANES, LANES), 1) // 8
    row_block = lax.broadcasted_iota(jnp.int32, (LANES, LANES), 0) // 8
    square[...] = jnp.where(lane_block >= row_block, upper, upper.T)
    kept = (row_at < hist) & (lax.broadcasted_iota(jnp.int32, (rows, LANES), 1) < hist)
    square[0:rows, :] = jnp.where(kept, square[0:rows, :], eye)
    square[0:base, :] = invert(square, base)
    square[0:rows, :] = jnp.where(kept, square[0:rows, :], 0.0)
    edges_wait(wide)

    solved, columns = [], []
    for iteration in range(ITERS):
        both = sums_of(iteration)
        proj, new = both[0:1, :], both[1:2, :]
        inverse = square[0:rows, :]
        proj_col, new_col = column_of(proj), column_of(new)
        proj_sol = jnp.broadcast_to(jnp.sum(inverse * proj, axis=1, keepdims=True), (rows, LANES))
        new_sol = jnp.broadcast_to(jnp.sum(inverse * new, axis=1, keepdims=True), (rows, LANES))
        solved.append(new_sol)
        columns.append(new_col)
        size = iteration + 1
        schur = [
            [columns[a][base + b : base + b + 1, :] - over_rows(columns[a] * solved[b]) for b in range(a + 1)]
            for a in range(size)
        ]
        right_side = [proj_col[base + a : base + a + 1, :] - over_rows(columns[a] * proj_sol) for a in range(size)]
        for a in range(size):
            for b in range(a + 1, size):
                factor = schur[b][a] / schur[a][a]
                right_side[b] = right_side[b] - factor * right_side[a]
                for c in range(a + 1, b + 1):
                    schur[b][c] = schur[b][c] - factor * schur[c][a]
        answer = [None] * size
        for a in reversed(range(size)):
            value = right_side[a]
            for b in range(a + 1, size):
                value = value - schur[b][a] * answer[b]
            answer[a] = value / schur[a][a]
        weights = proj_sol
        for a in range(size):
            weights = jnp.where(row_at == base + a, answer[a], weights - solved[a] * answer[a])

        def combine(at, carry):
            span = pl.ds(at * LANES if isinstance(at, int) else pl.multiple_of(at * LANES, LANES), LANES)
            total = new_w[:, span] * weights[base:rows, :]
            for first in range(0, hist, 8):
                some = min(8, hist - first)
                term = hist_w[first : first + some, span] * weights[first : first + some, :]
                if some < 8:
                    term = jnp.concatenate([term, jnp.zeros((8 - some, LANES), F32)], axis=0)
                total = total + term
            cur_x[:, span] = est_x[:, span] - over_rows(total)
            return carry

        lax.fori_loop(1, full // LANES - 1, combine, 0, unroll=4)
        if iteration + 1 < ITERS:
            combine(0, 0)
            combine(full // LANES - 1, 0)
            cur_x[...] = jnp.where(outside, 0.0, cur_x[...])
            begin(iteration + 1)
    next_ref[...] = cur_x[:, LANES : LANES + width]
    last_ref[...] = old_res[...]


def shards(n_iface, n_dom, *args):
    width = args[0].shape[0]
    hist = args[5].shape[0]
    base = -(-hist // 8) * 8
    rows = base + 8
    count = n_iface * n_dom
    pairs = (base // 8 + 1) // 2
    share = -(-pairs // n_dom)
    depth = next(d for d in (512, 256, 128) if width % d == 0)
    assert hist <= 112
    full = width + 2 * LANES
    vectors = [a.reshape(1, width) for a in args[:5]]
    any_spec = pl.BlockSpec(memory_space=pl.ANY)
    vmem_spec = pl.BlockSpec(memory_space=pltpu.VMEM)
    outs = pl.pallas_call(
        functools.partial(kernel, (n_iface, n_dom, hist, base, rows, width, share, depth)),
        out_shape=[pltpu.VMEM((1, width), F32)] * 2,
        in_specs=[any_spec] * 7,
        out_specs=[vmem_spec] * 2,
        scratch_shapes=[
            pltpu.VMEM((1, full), F32),
            pltpu.VMEM((1, full), F32),
            pltpu.VMEM((1, full), F32),
            pltpu.VMEM((1, full), F32),
            pltpu.VMEM((1, width), F32),
            pltpu.VMEM((hist, width), F32),
            pltpu.VMEM((hist, full), F32),
            pltpu.VMEM((8, width), F32),
            pltpu.VMEM((8, full), F32),
            pltpu.VMEM((ITERS, 2, LANES), F32),
            pltpu.VMEM((LANES, LANES), F32),
            pltpu.VMEM((n_dom, 8 * share, LANES), F32),
            pltpu.VMEM((n_dom, 8 * share, LANES), F32),
            pltpu.VMEM((n_iface, 8 * share, LANES), F32),
            pltpu.VMEM((n_dom, 8 * share, LANES), F32),
            pltpu.VMEM((ITERS, count, 2, LANES), F32),
            pltpu.SemaphoreType.DMA((width // depth,)),
            pltpu.SemaphoreType.DMA((6,)),
            pltpu.SemaphoreType.DMA((2, 4, 2)),
            pltpu.SemaphoreType.DMA((2, 1, 2)),
            pltpu.SemaphoreType.DMA((2,)),
            pltpu.SemaphoreType.DMA((2,)),
            pltpu.SemaphoreType.DMA((2,)),
            pltpu.SemaphoreType.DMA((ITERS, 2)),
        ],
        compiler_params=pltpu.CompilerParams(collective_id=0, has_side_effects=True),
        name="coupling",
    )(*vectors, args[5], args[6])

    def finish(a, b, c, d, sems):
        copies = [pltpu.make_async_copy(a, c, sems.at[0]), pltpu.make_async_copy(b, d, sems.at[1])]
        for copy in copies:
            copy.start()
        for copy in copies:
            copy.wait()

    outs = pl.pallas_call(
        finish,
        out_shape=[jax.ShapeDtypeStruct((1, width), F32)] * 2,
        in_specs=[vmem_spec] * 2,
        out_specs=[any_spec] * 2,
        scratch_shapes=[pltpu.SemaphoreType.DMA((2,))],
        name="finish",
    )(*[pltpu.with_memory_space_constraint(o, pltpu.VMEM) for o in outs])
    return outs[0].reshape(width), outs[1].reshape(width)


def solution(mesh):
    one = P(AXES)
    return jax.shard_map(
        functools.partial(shards, mesh.shape["iface"], mesh.shape["dom"]),
        mesh=mesh,
        in_specs=(one,) * 5 + (P(None, AXES),) * 2,
        out_specs=(one, one),
        check_vma=False,
    )
```

profile of v0, /device:TPU:0, one launch (start us, length us, event | category | flops | bytes accessed | tf_op | source)
XLA Modules:
  0.0 33.3 jit_solution(17774261696842907148)
XLA Ops:
  0.6 32.0 %coupling.1 = (f32[1,4096]{1,0:T(1,128)S(1)}, f32[1,4096]{1,0:T(1,128)S(1)}) custom-call(f32[1,4096]{1,0:T(1,128)} %bitcast.7, f32[1,4096]{1,0:T(1,128)} %bitcast.8, f32[1,4096]{1,0:T(1,128)} %bitcast.9, f32[1,4096]{1,0:T(1,128)} %bitcast.10, f32[1,4096]{1,0:T(1,128)} %bitcast.11, f32[100,4096]{1,0:T(8,128)} %history_residual.1, f32[100,4096]{1,0:T(8,128)} %history_estimate.1), custom_call_target="tpu_custom_call" | custom-call | tf_op jit(solution)/shard_map/coupling/pallas_call | solution.py:385
  32.6 0.6 %finish.1 = (f32[1,4096]{1,0:T(1,128)}, f32[1,4096]{1,0:T(1,128)}) custom-call(f32[1,4096]{1,0:T(1,128)S(1)} %get-tuple-element.6.a, f32[1,4096]{1,0:T(1,128)S(1)} %get-tuple-element.7.b), custom_call_target="tpu_custom_call" | custom-call | tf_op jit(solution)/shard_map/finish/pallas_call | solution.py:427
where the time goes:
time: 33.4 us; the launch traced here: 33.3 us
  Pallas kernels  32.6 us (98%)
  between operations  0.64 us (2%)
    pallas_call x1, Pallas kernels, shards(): pl.pallas_call(functools.partial(kernel, (n_iface, n_dom, hist, base, row...  32 us

commit v1 on v0

v1 whole, which is shorter than its diff:
```python
import functools
import jax
import jax.numpy as jnp
from jax import lax
from jax.experimental import pallas as pl
from jax.experimental.pallas import tpu as pltpu
from jax.sharding import PartitionSpec as P

ITERS = 3
coupling = 0.25
LANES = 128
AXES = ("iface", "dom")
F32 = jnp.float32
BF16 = jnp.bfloat16


def invert(matrix, rows):
    lane8 = lax.broadcasted_iota(jnp.int32, (8, LANES), 1)
    sub8 = lax.broadcasted_iota(jnp.int32, (8, LANES), 0)
    blocks = [matrix[8 * at : 8 * at + 8, :] for at in range(rows // 8)]
    for step in range(rows // 8):
        first = 8 * step
        inside = (lane8 >= first) & (lane8 < first + 8)
        unit = (lane8 - first == sub8).astype(F32)
        pivots = blocks[step]
        columns = [jnp.broadcast_to(pivots[:, first + at : first + at + 1], (8, LANES)) for at in range(8)]
        panel = jnp.where(inside, unit, pivots)
        for at in range(8):
            inverse = 1.0 / columns[at][at : at + 1, :]
            own = sub8 == at
            factor = columns[at]
            row = panel[at : at + 1, :] * inverse
            panel = jnp.where(own, row, panel - factor * row)
            for later in range(at + 1, 8):
                row = columns[later][at : at + 1, :] * inverse
                columns[later] = jnp.where(own, row, columns[later] - factor * row)
        for other in range(rows // 8):
            if other != step:
                block = blocks[other]
                total = jnp.where(inside, 0.0, block)
                for at in range(8):
                    column = jnp.broadcast_to(block[:, first + at : first + at + 1], (8, LANES))
                    total = total - column * panel[at : at + 1, :]
                blocks[other] = total
        blocks[step] = panel
    return jnp.concatenate(blocks, axis=0)


def kernel(
    sizes,
    interface,
    previous_residual,
    previous_estimate,
    forcing,
    stiffness,
    history_residual,
    history_estimate,
    next_ref,
    last_ref,
    cur,
    est,
    force,
    stiff,
    old_res,
    hist_v,
    hist_w,
    halo_w,
    new_v,
    new_w,
    edge_out,
    edge_in,
    dots_in,
    square,
    part_out,
    part_in,
    gathered,
    first_in,
    row_in,
    piece_sem,
    load_sem,
    edge_sem,
    wide_sem,
    part_sem,
    gather_sem,
    row_sem,
    go_sem,
):
    n_iface, n_dom, hist, base, rows, width, owners, share, depth = sizes
    count = n_iface * n_dom
    groups = width // LANES
    tall = groups + 8
    at_iface, at_dom = lax.axis_index("iface"), lax.axis_index("dom")
    me = at_iface * n_dom + at_dom
    last = count - 1
    n_own = len(owners)
    ifaces = [lax.rem(at_iface + step, n_iface) for step in range(n_iface)]
    doms = [lax.rem(at_dom + step, n_dom) for step in range(n_dom)]
    everyone = [(a, b) for a in ifaces for b in doms][1:]
    mine = [(at_iface == a) & (at_dom == b) for a, b in owners]
    owner = functools.reduce(jnp.logical_or, mine)
    slot = sum(jnp.where(yes, at, 0) for at, yes in enumerate(mine))

    def place(index):
        return (index // n_dom, lax.rem(index, n_dom))

    right = place(lax.rem(me + 1, count))
    left = place(lax.rem(me + last, count))

    def piece(at):
        span = pl.ds(at * depth, depth)
        return pltpu.make_async_copy(history_residual.at[:, span], hist_v.at[:, span], piece_sem.at[at])

    for at in range(width // depth):
        piece(at).start()
    inside = pl.ds(0, groups)
    small = []
    for at, (source, target) in enumerate(
        [
            (interface, cur.at[inside]),
            (previous_estimate, est.at[inside]),
            (forcing, force.at[inside]),
            (stiffness, stiff.at[inside]),
            (previous_residual, old_res),
        ]
    ):
        copy = pltpu.make_async_copy(source, target, load_sem.at[1 + at])
        copy.start()
        small.append(copy)
    load_w = pltpu.make_async_copy(history_estimate, hist_w, load_sem.at[0])

    barrier = pltpu.get_barrier_semaphore()

    def greet(device):
        pl.semaphore_signal(barrier, inc=1, device_id=device, device_id_type=pl.DeviceIdType.MESH)

    greet(right)
    greet(left)

    @pl.when(owner)
    def _():
        for device in everyone:
            greet(device)

    @pl.when(jnp.logical_not(owner))
    def _():
        for device in owners:
            greet(device)

    main = side = None
    dims = (((1,), (1,)), ((), ()))
    for at in range(width // depth):
        piece(at).wait()
        block = hist_v[:, at * depth : (at + 1) * depth]
        one = block.astype(BF16)
        rest = block - one.astype(F32)
        two = rest.astype(BF16)
        three = (rest - two.astype(F32)).astype(BF16)
        for a, b, which in [(one, one, 0), (two, two, 0), (two, one, 1), (three, one, 1)]:
            term = lax.dot_general(a, b, dims, preferred_element_type=F32)
            if which == 0:
                main = term if main is None else main + term
            else:
                side = term if side is None else side + term
    load_w.start()
    square[...] = jnp.zeros(square.shape, F32)
    square[0:hist, 0:hist] = side
    mirrored = square[...].T
    square[0:hist, 0:hist] = main + side
    square[...] = square[...] + mirrored
    lane8 = lax.broadcasted_iota(jnp.int32, (8, LANES), 1)
    sub8 = lax.broadcasted_iota(jnp.int32, (8, LANES), 0)
    blocks = (base // 8 + 1) // 2 * 2
    pairs = blocks // 2

    def natural(block):
        return (lane8 >= 8 * block) & (lane8 < 8 * blocks)

    for pair in range(n_own * share):
        where = (pair // share, pl.ds(8 * (pair % share), 8), slice(None))
        if pair < pairs:
            other = blocks - 1 - pair
            moved = pltpu.roll(square[8 * other : 8 * other + 8, :], 8 * pair + 8, 1)
            part_out[where] = jnp.where(natural(pair), square[8 * pair : 8 * pair + 8, :], moved)
        else:
            part_out[where] = jnp.zeros((8, LANES), F32)
    for copy in small:
        copy.wait()
    for at, ref in enumerate([cur, est, force, stiff]):
        edge_out[0, at : at + 1] = ref[groups - 1 : groups]
        edge_out[1, at : at + 1] = ref[0:1]
    pl.semaphore_wait(barrier, jnp.where(owner, last, n_own) + 2)

    def remote(source, target, send_sem, recv_sem, device):
        return pltpu.make_async_remote_copy(
            src_ref=source,
            dst_ref=target,
            send_sem=send_sem,
            recv_sem=recv_sem,
            device_id=device,
            device_id_type=pl.DeviceIdType.MESH,
        )

    def send(source, target, sems, device):
        remote(source, target, sems.at[0], sems.at[1], device).start()

    def drain(target, many, sem):
        most = target.at[pl.ds(0, many)]
        pltpu.make_async_copy(most, most, sem).wait()

    def edges(sources, target, sems):
        return [
            remote(source, target.at[side], sems.at[0, side], sems.at[1, side], device)
            for side, (source, device) in enumerate(zip(sources, [right, left]))
        ]

    def edges_start(copies):
        for side, some in enumerate([me < last, me > 0]):

            @pl.when(some)
            def _():
                copies[side].start()

    def edges_wait(copies):
        for side, (sent, received) in enumerate([(me < last, me > 0), (me > 0, me < last)]):

            @pl.when(sent)
            def _():
                copies[side].wait_send()

            @pl.when(received)
            def _():
                copies[side].wait_recv()

    for at, yes in enumerate(mine):

        @pl.when(yes)
        def _():
            part_in[me] = part_out[at]

        @pl.when(jnp.logical_not(yes))
        def _():
            send(part_out.at[at], part_in.at[me], part_sem, owners[at])

    @pl.when(mine[0])
    def _():
        for device in everyone:
            pl.semaphore_signal(go_sem, inc=1, device_id=device, device_id_type=pl.DeviceIdType.MESH)

    halos = edges([edge_out.at[0], edge_out.at[1]], edge_in, edge_sem)
    edges_start(halos)
    tail = pl.ds(width - LANES, LANES)
    head = pl.ds(0, LANES)
    wide = edges([hist_w.at[:, tail], hist_w.at[:, head]], halo_w, wide_sem)

    half = LANES // 2
    from_right = lane8 < half
    valid = (from_right & (me < last)) | ((lane8 >= half) & (me > 0))
    row_at = lax.broadcasted_iota(jnp.int32, (rows, LANES), 0)
    lane_at = lax.broadcasted_iota(jnp.int32, (rows, LANES), 1)
    eye = (row_at == lane_at).astype(F32)

    def column_of(row):
        return jnp.broadcast_to(jnp.sum(eye * row, axis=1, keepdims=True), (rows, LANES))

    def over_rows(value):
        return jnp.sum(value, axis=0, keepdims=True)

    def as_block(row):
        return jnp.broadcast_to(row, (8, LANES))

    def project(refs):
        def add(at, totals):
            first = pl.multiple_of(8 * at, 8)
            chunks = [ref[pl.ds(first, 8), :] for ref in refs]
            totals = list(totals)
            for inner in range(8):
                column = pl.ds(pl.multiple_of((8 * at + inner) * LANES, LANES), LANES)
                block = hist_v[:, column]
                for which, chunk in enumerate(chunks):
                    totals[which] = totals[which] + block * chunk[inner : inner + 1, :]
            return tuple(totals)

        zero = jnp.zeros((hist, LANES), F32)
        return lax.fori_loop(0, groups // 8, add, (zero,) * len(refs))

    def lane_sums(value):
        return over_rows(jnp.concatenate([value, jnp.zeros((LANES - value.shape[0], LANES), F32)], axis=0).T)

    def begin(iteration):
        if iteration == 0:
            totals_before = project([old_res])[0]
        current = cur[...]
        sides = []
        for shift, edge_lane in [(1, 0), (-1, LANES - 1)]:
            rolled = pltpu.roll(current, shift % LANES, 1)
            moved = pltpu.roll(rolled, shift % tall, 0)
            lane = lax.broadcasted_iota(jnp.int32, (tall, LANES), 1)
            sides.append(jnp.where(lane == edge_lane, moved, rolled))
        estimate = force[...] + stiff[...] * jnp.tanh(current) + coupling * (sides[0] + sides[1])
        new_w[iteration] = estimate - est[...]
        est[...] = estimate
        residual = (estimate - current)[0:groups]
        fresh = residual - old_res[...]
        new_v[iteration] = fresh
        old_res[...] = residual
        extra = jnp.zeros((8, LANES), F32)
        for other in range(iteration + 1):
            row = fresh if other == iteration else new_v[other]
            for first, value in [(0, residual), (4, fresh)]:
                extra = jnp.where(sub8 == first + other, over_rows(row * value), extra)
        total = project([old_res])[0]
        sums = lane_sums(jnp.concatenate([total, jnp.zeros((base - hist, LANES), F32), extra], axis=0))
        dots_in[iteration, 0:1] = sums
        target = row_in.at[iteration - 1]
        source = dots_in.at[iteration, pl.ds(0, 1)]
        if iteration == 0:
            dots_in[0, 1:2] = lane_sums(totals_before)
            target, source = first_in, dots_in.at[0]

            @pl.when(jnp.logical_not(mine[0]))
            def _():
                pl.semaphore_wait(go_sem, 1)

            first_in[me] = dots_in[0]
        else:
            row_in[iteration - 1, me] = sums
        for device in everyone:
            send(source, target.at[me], row_sem.at[iteration], device)

    def sums_of(iteration):
        target = first_in if iteration == 0 else row_in.at[iteration - 1]
        drain(target, last, row_sem.at[iteration, 1])
        return jnp.sum(target[...], axis=0)

    edges_wait(halos)
    for at, ref in enumerate([cur, est, force, stiff]):
        both = jnp.where(from_right, edge_in[1, at : at + 1], edge_in[0, at : at + 1])
        ref[groups:tall] = jnp.where(valid, both, 0.0)
    begin(0)
    load_w.wait()
    edges_start(wide)

    @pl.when(owner)
    def _():
        drain(part_in, last, part_sem.at[1])
        gathered[slot] = jnp.sum(part_in[...], axis=0)
        for device in everyone:
            send(gathered.at[slot], gathered.at[slot], gather_sem, device)
        drain(gathered, n_own - 1, gather_sem.at[1])

    @pl.when(jnp.logical_not(owner))
    def _():
        drain(gathered, n_own, gather_sem.at[1])

    for pair in range(pairs):
        other = blocks - 1 - pair
        packed = gathered[pair // share, pl.ds(8 * (pair % share), 8), :]
        square[8 * pair : 8 * pair + 8, :] = jnp.where(natural(pair), packed, 0.0)
        moved = pltpu.roll(packed, LANES - 8 * pair - 8, 1)
        square[8 * other : 8 * other + 8, :] = jnp.where(natural(other), moved, 0.0)
    upper = square[...]
    lane_block = lax.broadcasted_iota(jnp.int32, (LANES, LANES), 1) // 8
    row_block = lax.broadcasted_iota(jnp.int32, (LANES, LANES), 0) // 8
    square[...] = jnp.where(lane_block >= row_block, upper, upper.T)
    kept = (row_at < hist) & (lane_at < hist)
    square[0:rows, :] = jnp.where(kept, square[0:rows, :], eye)
    square[0:base, :] = invert(square, base)
    square[0:rows, :] = jnp.where(kept, square[0:rows, :], 0.0)
    edges_wait(wide)
    halo_w[0] = jnp.where(
        lax.broadcasted_iota(jnp.int32, (hist, LANES), 1) < half, halo_w[1], halo_w[0]
    )

    def fold(parts):
        for step in (1, 2, 4):
            low = lax.rem(sub8, 2 * step) < step
            parts = [
                jnp.where(low, a, b) + pltpu.roll(jnp.where(low, b, a), step, 0)
                for a, b in zip(parts[0::2], parts[1::2])
            ]
        return parts[0]

    def solve(row):
        return jnp.broadcast_to(jnp.sum(square[0:base, :] * row, axis=1, keepdims=True), (base, LANES))

    solved, columns, lower, scale = [], [], [], []
    for iteration in range(ITERS):
        both = sums_of(iteration)
        proj = both[0:1, :]
        proj_sol = solve(proj)
        proj_col = column_of(proj)
        extra = proj_col[base:rows]
        proj_col = proj_col[0:base]
        if iteration == 0:
            before_sol, before_col = solve(both[1:2, :]), column_of(both[1:2, :])[0:base]
        solved.append(proj_sol - before_sol)
        columns.append(proj_col - before_col)
        before_sol, before_col = proj_sol, proj_col
        size = iteration + 1
        ahead = []
        for b in range(size):
            value = extra[4 + b : 5 + b, :] - over_rows(columns[b] * solved[iteration])
            for c in range(b if b < iteration else 0):
                value = value - ahead[c] * lower[b][c]
            ahead.append(value)
        lower.append([ahead[b] * scale[b] for b in range(iteration)])
        pivot = ahead[iteration]
        for b in range(iteration):
            pivot = pivot - ahead[b] * lower[iteration][b]
        scale.append(1.0 / pivot)
        answer = []
        for a in range(size):
            value = extra[a : a + 1, :] - over_rows(solved[a] * proj_col)
            for b in range(a):
                value = value - lower[a][b] * answer[b]
            answer.append(value)
        answer = [value * scale[a] for a, value in enumerate(answer)]
        for a in reversed(range(size)):
            for b in range(a + 1, size):
                answer[a] = answer[a] - lower[b][a] * answer[b]
        weights = proj_sol
        for a in range(size):
            weights = weights - solved[a] * answer[a]

        def weighted(ref, column):
            total = None
            for first in range(0, hist, 8):
                some = min(8, hist - first)
                term = ref[first : first + some, column] * weights[first : first + some, :]
                if some < 8:
                    term = jnp.concatenate([term, jnp.zeros((8 - some, LANES), F32)], axis=0)
                total = term if total is None else total + term
            return total

        def finished(where, total):
            for a in range(size):
                total = total + new_w[a, where, :] * answer[a]
            return est[where, :] - total

        def combine(at, carry):
            parts = [
                weighted(hist_w, pl.ds(pl.multiple_of((8 * at + inner) * LANES, LANES), LANES)) for inner in range(8)
            ]
            where = pl.ds(pl.multiple_of(8 * at, 8), 8)
            cur[where, :] = finished(where, fold(parts))
            return carry

        lax.fori_loop(0, groups // 8, combine, 0)
        if iteration + 1 < ITERS:
            edge = as_block(over_rows(weighted(halo_w.at[0], slice(None))))
            cur[groups:tall] = jnp.where(valid, finished(pl.ds(groups, 8), edge), 0.0)
            begin(iteration + 1)
    next_ref[...] = cur[0:groups]
    last_ref[...] = old_res[...]

    @pl.when(owner)
    def _():
        drain(gathered, n_own - 1, part_sem.at[0])
        drain(part_in, last, gather_sem.at[0])

    @pl.when(jnp.logical_not(owner))
    def _():
        drain(gathered, n_own, part_sem.at[0])

    drain(first_in, last, row_sem.at[0, 0])
    for iteration in range(1, ITERS):
        drain(row_in.at[iteration - 1], last, row_sem.at[iteration, 0])


def shards(n_iface, n_dom, *args):
    width = args[0].shape[0]
    hist = args[5].shape[0]
    base = -(-hist // 8) * 8
    rows = base + 8
    count = n_iface * n_dom
    pairs = (base // 8 + 1) // 2
    middle = range(n_iface // 4, n_iface // 4 + max(1, n_iface // 2))
    owners = [(a, b) for a in middle for b in range(n_dom) if b % 2 == (n_dom > 1)][:pairs]
    share = -(-pairs // len(owners))
    depth = next(d for d in (2048, 1024) if width % d == 0)
    groups = width // LANES
    tall = groups + 8
    assert hist <= 112 and ITERS <= 4
    vectors = [a.reshape(groups, LANES) for a in args[:5]]
    any_spec = pl.BlockSpec(memory_space=pl.ANY)
    vmem_spec = pl.BlockSpec(memory_space=pltpu.VMEM)
    outs = pl.pallas_call(
        functools.partial(kernel, (n_iface, n_dom, hist, base, rows, width, owners, share, depth)),
        out_shape=[pltpu.VMEM((groups, LANES), F32)] * 2,
        in_specs=[any_spec] * 7,
        out_specs=[vmem_spec] * 2,
        scratch_shapes=[
            pltpu.VMEM((tall, LANES), F32),
            pltpu.VMEM((tall, LANES), F32),
            pltpu.VMEM((tall, LANES), F32),
            pltpu.VMEM((tall, LANES), F32),
            pltpu.VMEM((groups, LANES), F32),
            pltpu.VMEM((hist, width), F32),
            pltpu.VMEM((hist, width), F32),
            pltpu.VMEM((2, hist, LANES), F32),
            pltpu.VMEM((ITERS, groups, LANES), F32),
            pltpu.VMEM((ITERS, tall, LANES), F32),
            pltpu.VMEM((2, 8, LANES), F32),
            pltpu.VMEM((2, 8, LANES), F32),
            pltpu.VMEM((ITERS, 2, LANES), F32),
            pltpu.VMEM((LANES, LANES), F32),
            pltpu.VMEM((len(owners), 8 * share, LANES), F32),
            pltpu.VMEM((count, 8 * share, LANES), F32),
            pltpu.VMEM((len(owners), 8 * share, LANES), F32),
            pltpu.VMEM((count, 2, LANES), F32),
            pltpu.VMEM((ITERS - 1, count, 1, LANES), F32),
            pltpu.SemaphoreType.DMA((width // depth,)),
            pltpu.SemaphoreType.DMA((6,)),
            pltpu.SemaphoreType.DMA((2, 2)),
            pltpu.SemaphoreType.DMA((2, 2)),
            pltpu.SemaphoreType.DMA((2,)),
            pltpu.SemaphoreType.DMA((2,)),
            pltpu.SemaphoreType.DMA((ITERS, 2)),
            pltpu.SemaphoreType.REGULAR,
        ],
        compiler_params=pltpu.CompilerParams(collective_id=0, has_side_effects=True),
        name="coupling",
    )(*vectors, args[5], args[6])

    def finish(a, b, c, d, sems):
        copies = [pltpu.make_async_copy(a, c, sems.at[0]), pltpu.make_async_copy(b, d, sems.at[1])]
        for copy in copies:
            copy.start()
        for copy in copies:
            copy.wait()

    outs = pl.pallas_call(
        finish,
        out_shape=[jax.ShapeDtypeStruct((groups, LANES), F32)] * 2,
        in_specs=[vmem_spec] * 2,
        out_specs=[any_spec] * 2,
        scratch_shapes=[pltpu.SemaphoreType.DMA((2,))],
        name="finish",
    )(*[pltpu.with_memory_space_constraint(o, pltpu.VMEM) for o in outs])
    return outs[0].reshape(width), outs[1].reshape(width)


def solution(mesh):
    one = P(AXES)
    return jax.shard_map(
        functools.partial(shards, mesh.shape["iface"], mesh.shape["dom"]),
        mesh=mesh,
        in_specs=(one,) * 5 + (P(None, AXES),) * 2,
        out_specs=(one, one),
        check_vma=False,
    )
```

time: 33.4 us -> 29.3 us (0.88)
  Pallas kernels: 32.6 us -> 28.5 us
    pallas_call x1, Pallas kernels: 32 us -> 27.9 us  [shards(): pl.pallas_call(functools.partial(kernel, (n_iface, n_dom, hist, base, row...]
where the time goes in v1:
time: 29.3 us; the launch traced here: 29.1 us
  Pallas kernels  28.5 us (97%)
  between operations  0.64 us (2%)
    pallas_call x1, Pallas kernels, shards(): pl.pallas_call(functools.partial(kernel, (n_iface, n_dom, hist, base, row...  27.9 us
    pallas_call x1, Pallas kernels, shards(): pl.pallas_call(finish, out_shape=[jax.ShapeDtypeStruct((groups, LANES), F...  0.63 us

profile of v1, /device:TPU:0, one launch (start us, length us, event | category | flops | bytes accessed | tf_op | source)
XLA Modules:
  0.0 29.1 jit_solution(8486318758874621007)
XLA Ops:
  0.6 27.9 %coupling.1 = (f32[32,128]{1,0:T(8,128)S(1)}, f32[32,128]{1,0:T(8,128)S(1)}) custom-call(f32[32,128]{1,0:T(8,128)} %bitcast.7, f32[32,128]{1,0:T(8,128)} %bitcast.8, f32[32,128]{1,0:T(8,128)} %bitcast.9, f32[32,128]{1,0:T(8,128)} %bitcast.10, f32[32,128]{1,0:T(8,128)} %bitcast.11, f32[100,4096]{1,0:T(8,128)} %history_residual.1, f32[100,4096]{1,0:T(8,128)} %history_estimate.1), custom_call_target="tpu_custom_call" | custom-call | tf_op jit(solution)/shard_map/coupling/pallas_call | solution.py:487
  28.5 0.6 %finish.1 = (f32[32,128]{1,0:T(8,128)}, f32[32,128]{1,0:T(8,128)}) custom-call(f32[32,128]{1,0:T(8,128)S(1)} %get-tuple-element.6.a, f32[32,128]{1,0:T(8,128)S(1)} %get-tuple-element.7.b), custom_call_target="tpu_custom_call" | custom-call | tf_op jit(solution)/shard_map/finish/pallas_call | solution.py:532

commit v2 on v1

--- a/solution.py
+++ b/solution.py
@@ -93,9 +93,15 @@
     me = at_iface * n_dom + at_dom
     last = count - 1
     n_own = len(owners)
-    ifaces = [lax.rem(at_iface + step, n_iface) for step in range(n_iface)]
     doms = [lax.rem(at_dom + step, n_dom) for step in range(n_dom)]
-    everyone = [(a, b) for a in ifaces for b in doms][1:]
+    low = at_iface < n_iface // 2
+    others = []
+    for step in range(n_iface - 1):
+        down = n_iface - 1 - step
+        others.append(
+            jnp.where(low, jnp.where(down > at_iface, down, down - 1), jnp.where(step < at_iface, step, step + 1))
+        )
+    everyone = [(a, b) for a in others for b in doms] + [(at_iface, b) for b in doms[1:]]
     mine = [(at_iface == a) & (at_dom == b) for a, b in owners]
     owner = functools.reduce(jnp.logical_or, mine)
     slot = sum(jnp.where(yes, at, 0) for at, yes in enumerate(mine))
@@ -133,8 +139,13 @@
     def greet(device):
         pl.semaphore_signal(barrier, inc=1, device_id=device, device_id_type=pl.DeviceIdType.MESH)
 
-    greet(right)
-    greet(left)
+    @pl.when(me < last)
+    def _():
+        greet(right)
+
+    @pl.when(me > 0)
+    def _():
+        greet(left)
 
     @pl.when(owner)
     def _():
@@ -155,7 +166,7 @@
         rest = block - one.astype(F32)
         two = rest.astype(BF16)
         three = (rest - two.astype(F32)).astype(BF16)
-        for a, b, which in [(one, one, 0), (two, two, 0), (two, one, 1), (three, one, 1)]:
+        for a, b, which in [(two, one, 1), (three, one, 1), (one, one, 0), (two, two, 0)]:
             term = lax.dot_general(a, b, dims, preferred_element_type=F32)
             if which == 0:
                 main = term if main is None else main + term
@@ -169,26 +180,24 @@
     square[...] = square[...] + mirrored
     lane8 = lax.broadcasted_iota(jnp.int32, (8, LANES), 1)
     sub8 = lax.broadcasted_iota(jnp.int32, (8, LANES), 0)
-    blocks = (base // 8 + 1) // 2 * 2
-    pairs = blocks // 2
-
-    def natural(block):
-        return (lane8 >= 8 * block) & (lane8 < 8 * blocks)
+    blocks = base // 8
+    pairs = blocks // 2 + 1
+
+    def lanes_of(block):
+        return (lane8 >= 8 * block) & (lane8 < 8 * block + 8)
 
     for pair in range(n_own * share):
-        where = (pair // share, pl.ds(8 * (pair % share), 8), slice(None))
-        if pair < pairs:
-            other = blocks - 1 - pair
-            moved = pltpu.roll(square[8 * other : 8 * other + 8, :], 8 * pair + 8, 1)
-            part_out[where] = jnp.where(natural(pair), square[8 * pair : 8 * pair + 8, :], moved)
-        else:
-            part_out[where] = jnp.zeros((8, LANES), F32)
+        packed = jnp.zeros((8, LANES), F32)
+        for block in range(blocks if pair < pairs else 0):
+            shown = lanes_of((block - pair) % blocks)
+            packed = jnp.where(shown, square[8 * block : 8 * block + 8, :], packed)
+        part_out[pair // share, pl.ds(8 * (pair % share), 8), :] = packed
     for copy in small:
         copy.wait()
     for at, ref in enumerate([cur, est, force, stiff]):
         edge_out[0, at : at + 1] = ref[groups - 1 : groups]
         edge_out[1, at : at + 1] = ref[0:1]
-    pl.semaphore_wait(barrier, jnp.where(owner, last, n_own) + 2)
+    pl.semaphore_wait(barrier, jnp.where(owner, last, n_own) + jnp.where(me < last, 1, 0) + jnp.where(me > 0, 1, 0))
 
     def remote(source, target, send_sem, recv_sem, device):
         return pltpu.make_async_remote_copy(
@@ -272,16 +281,23 @@
         def add(at, totals):
             first = pl.multiple_of(8 * at, 8)
             chunks = [ref[pl.ds(first, 8), :] for ref in refs]
-            totals = list(totals)
-            for inner in range(8):
-                column = pl.ds(pl.multiple_of((8 * at + inner) * LANES, LANES), LANES)
-                block = hist_v[:, column]
+            totals = [list(some) for some in totals]
+            columns = pl.ds(pl.multiple_of(8 * LANES * at, 8 * LANES), 8 * LANES)
+            for group, first in enumerate(range(0, hist, 8)):
+                block = hist_v[first : min(first + 8, hist), columns]
                 for which, chunk in enumerate(chunks):
-                    totals[which] = totals[which] + block * chunk[inner : inner + 1, :]
-            return tuple(totals)
-
-        zero = jnp.zeros((hist, LANES), F32)
-        return lax.fori_loop(0, groups // 8, add, (zero,) * len(refs))
+                    terms = [
+                        block[:, inner * LANES : (inner + 1) * LANES] * chunk[inner : inner + 1, :]
+                        for inner in range(8)
+                    ]
+                    while len(terms) > 1:
+                        terms = [a + b for a, b in zip(terms[0::2], terms[1::2])]
+                    totals[which][group] = totals[which][group] + terms[0]
+            return totals
+
+        zeros = [jnp.zeros((min(8, hist - first), LANES), F32) for first in range(0, hist, 8)]
+        totals = lax.fori_loop(0, groups // 8, add, [list(zeros) for _ in refs])
+        return [jnp.concatenate(some, axis=0) for some in totals]
 
     def lane_sums(value):
         return over_rows(jnp.concatenate([value, jnp.zeros((LANES - value.shape[0], LANES), F32)], axis=0).T)
@@ -352,16 +368,19 @@
     def _():
         drain(gathered, n_own, gather_sem.at[1])
 
-    for pair in range(pairs):
-        other = blocks - 1 - pair
-        packed = gathered[pair // share, pl.ds(8 * (pair % share), 8), :]
-        square[8 * pair : 8 * pair + 8, :] = jnp.where(natural(pair), packed, 0.0)
-        moved = pltpu.roll(packed, LANES - 8 * pair - 8, 1)
-        square[8 * other : 8 * other + 8, :] = jnp.where(natural(other), moved, 0.0)
-    upper = square[...]
+    for block in range(blocks):
+        row = jnp.zeros((8, LANES), F32)
+        for pair in range(pairs):
+            packed = gathered[pair // share, pl.ds(8 * (pair % share), 8), :]
+            row = jnp.where(lanes_of((block - pair) % blocks), packed, row)
+        square[8 * block : 8 * block + 8, :] = row
+    square[base:LANES, :] = jnp.zeros((LANES - base, LANES), F32)
+    shown = square[...]
     lane_block = lax.broadcasted_iota(jnp.int32, (LANES, LANES), 1) // 8
     row_block = lax.broadcasted_iota(jnp.int32, (LANES, LANES), 0) // 8
-    square[...] = jnp.where(lane_block >= row_block, upper, upper.T)
+    ahead_by = row_block - lane_block
+    ahead_by = jnp.where(ahead_by < 0, ahead_by + blocks, ahead_by)
+    square[...] = jnp.where(ahead_by < pairs, shown, shown.T)
     kept = (row_at < hist) & (lane_at < hist)
     square[0:rows, :] = jnp.where(kept, square[0:rows, :], eye)
     square[0:base, :] = invert(square, base)
@@ -385,6 +404,20 @@
 
     solved, columns, lower, scale = [], [], [], []
     for iteration in range(ITERS):
+        if iteration == 1:
+
+            @pl.when(owner)
+            def _():
+                drain(gathered, n_own - 1, part_sem.at[0])
+                drain(part_in, last, gather_sem.at[0])
+
+            @pl.when(jnp.logical_not(owner))
+            def _():
+                drain(gathered, n_own, part_sem.at[0])
+
+            drain(first_in, last, row_sem.at[0, 0])
+        elif iteration > 1:
+            drain(row_in.at[iteration - 2], last, row_sem.at[iteration - 1, 0])
         both = sums_of(iteration)
         proj = both[0:1, :]
         proj_sol = solve(proj)
@@ -422,15 +455,17 @@
         for a in range(size):
             weights = weights - solved[a] * answer[a]
 
-        def weighted(ref, column):
-            total = None
-            for first in range(0, hist, 8):
+        def weighted(ref, columns, many):
+            totals = [None] * many
+            for first in reversed(range(0, hist, 8)):
                 some = min(8, hist - first)
-                term = ref[first : first + some, column] * weights[first : first + some, :]
-                if some < 8:
-                    term = jnp.concatenate([term, jnp.zeros((8 - some, LANES), F32)], axis=0)
-                total = term if total is None else total + term
-            return total
+                block = ref[first : first + some, columns]
+                for inner in range(many):
+                    term = block[:, inner * LANES : (inner + 1) * LANES] * weights[first : first + some, :]
+                    if some < 8:
+                        term = jnp.concatenate([term, jnp.zeros((8 - some, LANES), F32)], axis=0)
+                    totals[inner] = term if totals[inner] is None else totals[inner] + term
+            return totals
 
         def finished(where, total):
             for a in range(size):
@@ -438,33 +473,20 @@
             return est[where, :] - total
 
         def combine(at, carry):
-            parts = [
-                weighted(hist_w, pl.ds(pl.multiple_of((8 * at + inner) * LANES, LANES), LANES)) for inner in range(8)
-            ]
+            parts = weighted(hist_w, pl.ds(pl.multiple_of(8 * LANES * at, 8 * LANES), 8 * LANES), 8)
             where = pl.ds(pl.multiple_of(8 * at, 8), 8)
             cur[where, :] = finished(where, fold(parts))
             return carry
 
         lax.fori_loop(0, groups // 8, combine, 0)
         if iteration + 1 < ITERS:
-            edge = as_block(over_rows(weighted(halo_w.at[0], slice(None))))
+            edge = as_block(over_rows(weighted(halo_w.at[0], slice(None), 1)[0]))
             cur[groups:tall] = jnp.where(valid, finished(pl.ds(groups, 8), edge), 0.0)
             begin(iteration + 1)
     next_ref[...] = cur[0:groups]
     last_ref[...] = old_res[...]
 
-    @pl.when(owner)
-    def _():
-        drain(gathered, n_own - 1, part_sem.at[0])
-        drain(part_in, last, gather_sem.at[0])
-
-    @pl.when(jnp.logical_not(owner))
-    def _():
-        drain(gathered, n_own, part_sem.at[0])
-
-    drain(first_in, last, row_sem.at[0, 0])
-    for iteration in range(1, ITERS):
-        drain(row_in.at[iteration - 1], last, row_sem.at[iteration, 0])
+    drain(row_in.at[ITERS - 2], last, row_sem.at[ITERS - 1, 0])
 
 
 def shards(n_iface, n_dom, *args):
@@ -473,7 +495,7 @@
     base = -(-hist // 8) * 8
     rows = base + 8
     count = n_iface * n_dom
-    pairs = (base // 8 + 1) // 2
+    pairs = base // 8 // 2 + 1
     middle = range(n_iface // 4, n_iface // 4 + max(1, n_iface // 2))
     owners = [(a, b) for a in middle for b in range(n_dom) if b % 2 == (n_dom > 1)][:pairs]
     share = -(-pairs // len(owners))

time: 29.3 us -> 28.4 us (0.969)
  Pallas kernels: 28.5 us -> 27.6 us
    pallas_call x1, Pallas kernels: 27.9 us -> 26.9 us  [shards(): pl.pallas_call(functools.partial(kernel, (n_iface, n_dom, hist, base, row...]
where the time goes in v2:
time: 28.4 us; the launch traced here: 28.2 us
  Pallas kernels  27.6 us (97%)
  between operations  0.64 us (2%)
    pallas_call x1, Pallas kernels, shards(): pl.pallas_call(functools.partial(kernel, (n_iface, n_dom, hist, base, row...  26.9 us
    pallas_call x1, Pallas kernels, shards(): pl.pallas_call(finish, out_shape=[jax.ShapeDtypeStruct((groups, LANES), F...  0.63 us

profile of v2, /device:TPU:0, one launch (start us, length us, event | category | flops | bytes accessed | tf_op | source)
XLA Modules:
  0.0 28.2 jit_solution(2842014507956593913)
XLA Ops:
  0.6 26.9 %coupling.1 = (f32[32,128]{1,0:T(8,128)S(1)}, f32[32,128]{1,0:T(8,128)S(1)}) custom-call(f32[32,128]{1,0:T(8,128)} %bitcast.7, f32[32,128]{1,0:T(8,128)} %bitcast.8, f32[32,128]{1,0:T(8,128)} %bitcast.9, f32[32,128]{1,0:T(8,128)} %bitcast.10, f32[32,128]{1,0:T(8,128)} %bitcast.11, f32[100,4096]{1,0:T(8,128)} %history_residual.1, f32[100,4096]{1,0:T(8,128)} %history_estimate.1), custom_call_target="tpu_custom_call" | custom-call | tf_op jit(solution)/shard_map/coupling/pallas_call | solution.py:509
  27.6 0.6 %finish.1 = (f32[32,128]{1,0:T(8,128)}, f32[32,128]{1,0:T(8,128)}) custom-call(f32[32,128]{1,0:T(8,128)S(1)} %get-tuple-element.6.a, f32[32,128]{1,0:T(8,128)S(1)} %get-tuple-element.7.b), custom_call_target="tpu_custom_call" | custom-call | tf_op jit(solution)/shard_map/finish/pallas_call | solution.py:554

commit v3 on v2

--- a/solution.py
+++ b/solution.py
@@ -17,14 +17,21 @@
 def invert(matrix, rows):
     lane8 = lax.broadcasted_iota(jnp.int32, (8, LANES), 1)
     sub8 = lax.broadcasted_iota(jnp.int32, (8, LANES), 0)
-    blocks = [matrix[8 * at : 8 * at + 8, :] for at in range(rows // 8)]
-    for step in range(rows // 8):
+    many = rows // 8
+    blocks = [matrix[8 * at : 8 * at + 8, :] for at in range(many)]
+    def spread(block, lane):
+        return jnp.broadcast_to(jnp.sum(jnp.where(lane8 == lane, block, 0.0), axis=1, keepdims=True), (8, LANES))
+    columns = [spread(blocks[0], at) for at in range(8)]
+    for step in range(many):
         first = 8 * step
         inside = (lane8 >= first) & (lane8 < first + 8)
         unit = (lane8 - first == sub8).astype(F32)
-        pivots = blocks[step]
-        columns = [jnp.broadcast_to(pivots[:, first + at : first + at + 1], (8, LANES)) for at in range(8)]
-        panel = jnp.where(inside, unit, pivots)
+        panel = jnp.where(inside, unit, blocks[step])
+        factors = [None if other == step else [spread(blocks[other], first + at) for at in range(8)] for other in range(many)]
+        ahead = step + 1 < many
+        if ahead:
+            below = list(factors[step + 1])
+            corner = [spread(blocks[step + 1], first + 8 + at) for at in range(8)]
         for at in range(8):
             inverse = 1.0 / columns[at][at : at + 1, :]
             own = sub8 == at
@@ -34,15 +41,25 @@
             for later in range(at + 1, 8):
                 row = columns[later][at : at + 1, :] * inverse
                 columns[later] = jnp.where(own, row, columns[later] - factor * row)
-        for other in range(rows // 8):
+                if ahead:
+                    below[later] = below[later] - below[at] * row
+            if ahead:
+                scaled = below[at] * inverse
+                for c in range(8):
+                    corner[c] = corner[c] - below[at] * scaled[c : c + 1, :]
+        for other in range(many):
             if other != step:
-                block = blocks[other]
-                total = jnp.where(inside, 0.0, block)
-                for at in range(8):
-                    column = jnp.broadcast_to(block[:, first + at : first + at + 1], (8, LANES))
-                    total = total - column * panel[at : at + 1, :]
+                total = jnp.where(inside, 0.0, blocks[other])
+                terms = [factors[other][at] * panel[at : at + 1, :] for at in range(8)]
+                if True:
+                    while len(terms) > 1:
+                        terms = [a + b for a, b in zip(terms[0::2], terms[1::2])]
+                for term in terms:
+                    total = total - term
                 blocks[other] = total
         blocks[step] = panel
+        if ahead:
+            columns = corner
     return jnp.concatenate(blocks, axis=0)
 
 
@@ -85,7 +102,7 @@
     row_sem,
     go_sem,
 ):
-    n_iface, n_dom, hist, base, rows, width, owners, share, depth = sizes
+    n_iface, n_dom, hist, base, rows, width, owners, share, depths = sizes
     count = n_iface * n_dom
     groups = width // LANES
     tall = groups + 8
@@ -113,10 +130,10 @@
     left = place(lax.rem(me + last, count))
 
     def piece(at):
-        span = pl.ds(at * depth, depth)
+        span = pl.ds(sum(depths[:at]), depths[at])
         return pltpu.make_async_copy(history_residual.at[:, span], hist_v.at[:, span], piece_sem.at[at])
 
-    for at in range(width // depth):
+    for at in range(len(depths)):
         piece(at).start()
     inside = pl.ds(0, groups)
     small = []
@@ -159,9 +176,9 @@
 
     main = side = None
     dims = (((1,), (1,)), ((), ()))
-    for at in range(width // depth):
+    for at in range(len(depths)):
         piece(at).wait()
-        block = hist_v[:, at * depth : (at + 1) * depth]
+        block = hist_v[:, sum(depths[:at]) : sum(depths[: at + 1])]
         one = block.astype(BF16)
         rest = block - one.astype(F32)
         two = rest.astype(BF16)
@@ -279,10 +296,10 @@
 
     def project(refs):
         def add(at, totals):
-            first = pl.multiple_of(8 * at, 8)
+            first = 8 * at
             chunks = [ref[pl.ds(first, 8), :] for ref in refs]
             totals = [list(some) for some in totals]
-            columns = pl.ds(pl.multiple_of(8 * LANES * at, 8 * LANES), 8 * LANES)
+            columns = pl.ds(8 * LANES * at, 8 * LANES)
             for group, first in enumerate(range(0, hist, 8)):
                 block = hist_v[first : min(first + 8, hist), columns]
                 for which, chunk in enumerate(chunks):
@@ -296,7 +313,9 @@
             return totals
 
         zeros = [jnp.zeros((min(8, hist - first), LANES), F32) for first in range(0, hist, 8)]
-        totals = lax.fori_loop(0, groups // 8, add, [list(zeros) for _ in refs])
+        totals = [list(zeros) for _ in refs]
+        for at in range(groups // 8):
+            totals = add(at, totals)
         return [jnp.concatenate(some, axis=0) for some in totals]
 
     def lane_sums(value):
@@ -355,13 +374,19 @@
     begin(0)
     load_w.wait()
     edges_start(wide)
-
     @pl.when(owner)
     def _():
         drain(part_in, last, part_sem.at[1])
         gathered[slot] = jnp.sum(part_in[...], axis=0)
         for device in everyone:
             send(gathered.at[slot], gathered.at[slot], gather_sem, device)
+
+    both = sums_of(0)
+    row_first, row_before = both[0:1, :], both[1:2, :]
+    col_first, col_before = column_of(row_first), column_of(row_before)[0:base]
+
+    @pl.when(owner)
+    def _():
         drain(gathered, n_own - 1, gather_sem.at[1])
 
     @pl.when(jnp.logical_not(owner))
@@ -418,14 +443,15 @@
             drain(first_in, last, row_sem.at[0, 0])
         elif iteration > 1:
             drain(row_in.at[iteration - 2], last, row_sem.at[iteration - 1, 0])
-        both = sums_of(iteration)
-        proj = both[0:1, :]
+        if iteration == 0:
+            proj, proj_col, before_col = row_first, col_first, col_before
+            before_sol = solve(row_before)
+        else:
+            proj = sums_of(iteration)
+            proj_col = column_of(proj)
         proj_sol = solve(proj)
-        proj_col = column_of(proj)
         extra = proj_col[base:rows]
         proj_col = proj_col[0:base]
-        if iteration == 0:
-            before_sol, before_col = solve(both[1:2, :]), column_of(both[1:2, :])[0:base]
         solved.append(proj_sol - before_sol)
         columns.append(proj_col - before_col)
         before_sol, before_col = proj_sol, proj_col
@@ -473,12 +499,13 @@
             return est[where, :] - total
 
         def combine(at, carry):
-            parts = weighted(hist_w, pl.ds(pl.multiple_of(8 * LANES * at, 8 * LANES), 8 * LANES), 8)
-            where = pl.ds(pl.multiple_of(8 * at, 8), 8)
+            parts = weighted(hist_w, pl.ds(8 * LANES * at, 8 * LANES), 8)
+            where = pl.ds(8 * at, 8)
             cur[where, :] = finished(where, fold(parts))
             return carry
 
-        lax.fori_loop(0, groups // 8, combine, 0)
+        for at in range(groups // 8):
+            combine(at, 0)
         if iteration + 1 < ITERS:
             edge = as_block(over_rows(weighted(halo_w.at[0], slice(None), 1)[0]))
             cur[groups:tall] = jnp.where(valid, finished(pl.ds(groups, 8), edge), 0.0)
@@ -499,7 +526,9 @@
     middle = range(n_iface // 4, n_iface // 4 + max(1, n_iface // 2))
     owners = [(a, b) for a in middle for b in range(n_dom) if b % 2 == (n_dom > 1)][:pairs]
     share = -(-pairs // len(owners))
-    depth = next(d for d in (2048, 1024) if width % d == 0)
+    assert width % (8 * LANES) == 0
+    quarter = max(LANES, width // 4 // LANES * LANES)
+    depths = [quarter, quarter, width - 2 * quarter]
     groups = width // LANES
     tall = groups + 8
     assert hist <= 112 and ITERS <= 4
@@ -507,7 +536,7 @@
     any_spec = pl.BlockSpec(memory_space=pl.ANY)
     vmem_spec = pl.BlockSpec(memory_space=pltpu.VMEM)
     outs = pl.pallas_call(
-        functools.partial(kernel, (n_iface, n_dom, hist, base, rows, width, owners, share, depth)),
+        functools.partial(kernel, (n_iface, n_dom, hist, base, rows, width, owners, share, depths)),
         out_shape=[pltpu.VMEM((groups, LANES), F32)] * 2,
         in_specs=[any_spec] * 7,
         out_specs=[vmem_spec] * 2,
@@ -531,7 +560,7 @@
             pltpu.VMEM((len(owners), 8 * share, LANES), F32),
             pltpu.VMEM((count, 2, LANES), F32),
             pltpu.VMEM((ITERS - 1, count, 1, LANES), F32),
-            pltpu.SemaphoreType.DMA((width // depth,)),
+            pltpu.SemaphoreType.DMA((len(depths),)),
             pltpu.SemaphoreType.DMA((6,)),
             pltpu.SemaphoreType.DMA((2, 2)),
             pltpu.SemaphoreType.DMA((2, 2)),

time: 28.4 us -> 27.3 us (0.961)
  Pallas kernels: 27.6 us -> 26.5 us
    pallas_call x1, Pallas kernels: 26.9 us -> 25.9 us  [shards(): pl.pallas_call(functools.partial(kernel, (n_iface, n_dom, hist, base, row...]
where the time goes in v3:
time: 27.3 us; the launch traced here: 27.2 us
  Pallas kernels  26.5 us (97%)
  between operations  0.64 us (2%)
    pallas_call x1, Pallas kernels, shards(): pl.pallas_call(functools.partial(kernel, (n_iface, n_dom, hist, base, row...  25.9 us
    pallas_call x1, Pallas kernels, shards(): pl.pallas_call(finish, out_shape=[jax.ShapeDtypeStruct((groups, LANES), F...  0.63 us

profile of v3, /device:TPU:0, one launch (start us, length us, event | category | flops | bytes accessed | tf_op | source)
XLA Modules:
  0.0 27.2 jit_solution(8280098867229300019)
XLA Ops:
  0.6 25.9 %coupling.1 = (f32[32,128]{1,0:T(8,128)S(1)}, f32[32,128]{1,0:T(8,128)S(1)}) custom-call(f32[32,128]{1,0:T(8,128)} %bitcast.7, f32[32,128]{1,0:T(8,128)} %bitcast.8, f32[32,128]{1,0:T(8,128)} %bitcast.9, f32[32,128]{1,0:T(8,128)} %bitcast.10, f32[32,128]{1,0:T(8,128)} %bitcast.11, f32[100,4096]{1,0:T(8,128)} %history_residual.1, f32[100,4096]{1,0:T(8,128)} %history_estimate.1), custom_call_target="tpu_custom_call" | custom-call | tf_op jit(solution)/shard_map/coupling/pallas_call | solution.py:538
  26.5 0.6 %finish.1 = (f32[32,128]{1,0:T(8,128)}, f32[32,128]{1,0:T(8,128)}) custom-call(f32[32,128]{1,0:T(8,128)S(1)} %get-tuple-element.6.a, f32[32,128]{1,0:T(8,128)S(1)} %get-tuple-element.7.b), custom_call_target="tpu_custom_call" | custom-call | tf_op jit(solution)/shard_map/finish/pallas_call | solution.py:583

commit v4 on v3

--- a/solution.py
+++ b/solution.py
@@ -97,6 +97,7 @@
     load_sem,
     edge_sem,
     wide_sem,
+    sent_sem,
     part_sem,
     gather_sem,
     row_sem,
@@ -136,8 +137,7 @@
     for at in range(len(depths)):
         piece(at).start()
     inside = pl.ds(0, groups)
-    small = []
-    for at, (source, target) in enumerate(
+    for source, target in (
         [
             (interface, cur.at[inside]),
             (previous_estimate, est.at[inside]),
@@ -146,10 +146,8 @@
             (previous_residual, old_res),
         ]
     ):
-        copy = pltpu.make_async_copy(source, target, load_sem.at[1 + at])
-        copy.start()
-        small.append(copy)
-    load_w = pltpu.make_async_copy(history_estimate, hist_w, load_sem.at[0])
+        pltpu.make_async_copy(source, target, load_sem).start()
+    load_w = pltpu.make_async_copy(history_estimate, hist_w, piece_sem.at[0])
 
     barrier = pltpu.get_barrier_semaphore()
 
@@ -209,8 +207,8 @@
             shown = lanes_of((block - pair) % blocks)
             packed = jnp.where(shown, square[8 * block : 8 * block + 8, :], packed)
         part_out[pair // share, pl.ds(8 * (pair % share), 8), :] = packed
-    for copy in small:
-        copy.wait()
+    together = hist_v.at[pl.ds(0, 8), pl.ds(0, 5 * width // 8)]
+    pltpu.make_async_copy(together, together, load_sem).wait()
     for at, ref in enumerate([cur, est, force, stiff]):
         edge_out[0, at : at + 1] = ref[groups - 1 : groups]
         edge_out[1, at : at + 1] = ref[0:1]
@@ -226,16 +224,16 @@
             device_id_type=pl.DeviceIdType.MESH,
         )
 
-    def send(source, target, sems, device):
-        remote(source, target, sems.at[0], sems.at[1], device).start()
+    def send(source, target, sem, device):
+        remote(source, target, sent_sem, sem, device).start()
 
     def drain(target, many, sem):
         most = target.at[pl.ds(0, many)]
         pltpu.make_async_copy(most, most, sem).wait()
 
-    def edges(sources, target, sems):
+    def edges(sources, target, sem):
         return [
-            remote(source, target.at[side], sems.at[0, side], sems.at[1, side], device)
+            remote(source, target.at[side], edge_sem.at[0, side], sem.at[side], device)
             for side, (source, device) in enumerate(zip(sources, [right, left]))
         ]
 
@@ -272,7 +270,7 @@
         for device in everyone:
             pl.semaphore_signal(go_sem, inc=1, device_id=device, device_id_type=pl.DeviceIdType.MESH)
 
-    halos = edges([edge_out.at[0], edge_out.at[1]], edge_in, edge_sem)
+    halos = edges([edge_out.at[0], edge_out.at[1]], edge_in, edge_sem.at[1])
     edges_start(halos)
     tail = pl.ds(width - LANES, LANES)
     head = pl.ds(0, LANES)
@@ -359,12 +357,30 @@
             first_in[me] = dots_in[0]
         else:
             row_in[iteration - 1, me] = sums
+        if iteration == 0:
+
+            @pl.when(owner)
+            def _():
+                drain(gathered, n_own - 1, sent_sem)
+
+            @pl.when(jnp.logical_not(owner))
+            def _():
+                drain(gathered, n_own, sent_sem)
+
+        elif iteration == 1:
+
+            @pl.when(owner)
+            def _():
+                drain(part_in, last, sent_sem)
+
+        else:
+            drain(row_in.at[iteration - 2], last, sent_sem)
         for device in everyone:
-            send(source, target.at[me], row_sem.at[iteration], device)
+            send(source, target.at[me], row_sem.at[iteration % 2], device)
 
     def sums_of(iteration):
         target = first_in if iteration == 0 else row_in.at[iteration - 1]
-        drain(target, last, row_sem.at[iteration, 1])
+        drain(target, last, row_sem.at[iteration % 2])
         return jnp.sum(target[...], axis=0)
 
     edges_wait(halos)
@@ -374,9 +390,10 @@
     begin(0)
     load_w.wait()
     edges_start(wide)
+    drain(first_in, last, sent_sem)
     @pl.when(owner)
     def _():
-        drain(part_in, last, part_sem.at[1])
+        drain(part_in, last, part_sem)
         gathered[slot] = jnp.sum(part_in[...], axis=0)
         for device in everyone:
             send(gathered.at[slot], gathered.at[slot], gather_sem, device)
@@ -387,11 +404,11 @@
 
     @pl.when(owner)
     def _():
-        drain(gathered, n_own - 1, gather_sem.at[1])
+        drain(gathered, n_own - 1, gather_sem)
 
     @pl.when(jnp.logical_not(owner))
     def _():
-        drain(gathered, n_own, gather_sem.at[1])
+        drain(gathered, n_own, gather_sem)
 
     for block in range(blocks):
         row = jnp.zeros((8, LANES), F32)
@@ -429,20 +446,6 @@
 
     solved, columns, lower, scale = [], [], [], []
     for iteration in range(ITERS):
-        if iteration == 1:
-
-            @pl.when(owner)
-            def _():
-                drain(gathered, n_own - 1, part_sem.at[0])
-                drain(part_in, last, gather_sem.at[0])
-
-            @pl.when(jnp.logical_not(owner))
-            def _():
-                drain(gathered, n_own, part_sem.at[0])
-
-            drain(first_in, last, row_sem.at[0, 0])
-        elif iteration > 1:
-            drain(row_in.at[iteration - 2], last, row_sem.at[iteration - 1, 0])
         if iteration == 0:
             proj, proj_col, before_col = row_first, col_first, col_before
             before_sol = solve(row_before)
@@ -513,7 +516,7 @@
     next_ref[...] = cur[0:groups]
     last_ref[...] = old_res[...]
 
-    drain(row_in.at[ITERS - 2], last, row_sem.at[ITERS - 1, 0])
+    drain(row_in.at[ITERS - 2], last, sent_sem)
 
 
 def shards(n_iface, n_dom, *args):
@@ -561,12 +564,13 @@
             pltpu.VMEM((count, 2, LANES), F32),
             pltpu.VMEM((ITERS - 1, count, 1, LANES), F32),
             pltpu.SemaphoreType.DMA((len(depths),)),
-            pltpu.SemaphoreType.DMA((6,)),
-            pltpu.SemaphoreType.DMA((2, 2)),
+            pltpu.SemaphoreType.DMA,
             pltpu.SemaphoreType.DMA((2, 2)),
             pltpu.SemaphoreType.DMA((2,)),
+            pltpu.SemaphoreType.DMA,
+            pltpu.SemaphoreType.DMA,
+            pltpu.SemaphoreType.DMA,
             pltpu.SemaphoreType.DMA((2,)),
-            pltpu.SemaphoreType.DMA((ITERS, 2)),
             pltpu.SemaphoreType.REGULAR,
         ],
         compiler_params=pltpu.CompilerParams(collective_id=0, has_side_effects=True),

time: 27.3 us -> 27.2 us (level)
  no operation moved by 1% of the time
where the time goes in v4:
time: 27.2 us; the launch traced here: 27.1 us
  Pallas kernels  26.4 us (97%)
  between operations  0.64 us (2%)
    pallas_call x1, Pallas kernels, shards(): pl.pallas_call(functools.partial(kernel, (n_iface, n_dom, hist, base, row...  25.8 us
    pallas_call x1, Pallas kernels, shards(): pl.pallas_call(finish, out_shape=[jax.ShapeDtypeStruct((groups, LANES), F...  0.63 us

profile of v4, /device:TPU:0, one launch (start us, length us, event | category | flops | bytes accessed | tf_op | source)
XLA Modules:
  0.0 27.1 jit_solution(8522285102605070305)
XLA Ops:
  0.6 25.8 %coupling.1 = (f32[32,128]{1,0:T(8,128)S(1)}, f32[32,128]{1,0:T(8,128)S(1)}) custom-call(f32[32,128]{1,0:T(8,128)} %bitcast.7, f32[32,128]{1,0:T(8,128)} %bitcast.8, f32[32,128]{1,0:T(8,128)} %bitcast.9, f32[32,128]{1,0:T(8,128)} %bitcast.10, f32[32,128]{1,0:T(8,128)} %bitcast.11, f32[100,4096]{1,0:T(8,128)} %history_residual.1, f32[100,4096]{1,0:T(8,128)} %history_estimate.1), custom_call_target="tpu_custom_call" | custom-call | tf_op jit(solution)/shard_map/coupling/pallas_call | solution.py:541
  26.4 0.6 %finish.1 = (f32[32,128]{1,0:T(8,128)}, f32[32,128]{1,0:T(8,128)}) custom-call(f32[32,128]{1,0:T(8,128)S(1)} %get-tuple-element.6.a, f32[32,128]{1,0:T(8,128)S(1)} %get-tuple-element.7.b), custom_call_target="tpu_custom_call" | custom-call | tf_op jit(solution)/shard_map/finish/pallas_call | solution.py:587

commit v5 on v4

--- a/solution.py
+++ b/solution.py
@@ -527,7 +527,7 @@
     count = n_iface * n_dom
     pairs = base // 8 // 2 + 1
     middle = range(n_iface // 4, n_iface // 4 + max(1, n_iface // 2))
-    owners = [(a, b) for a in middle for b in range(n_dom) if b % 2 == (n_dom > 1)][:pairs]
+    owners = [(a, b) for a in reversed(middle) for b in range(n_dom) if b % 2 == (n_dom > 1)][:pairs]
     share = -(-pairs // len(owners))
     assert width % (8 * LANES) == 0
     quarter = max(LANES, width // 4 // LANES * LANES)

time: 27.2 us -> 27.8 us (1.022)
  Pallas kernels: 26.4 us -> 27 us
    pallas_call x1, Pallas kernels: 25.8 us -> 26.4 us  [shards(): pl.pallas_call(functools.partial(kernel, (n_iface, n_dom, hist, base, row...]
where the time goes in v5:
time: 27.8 us; the launch traced here: 27.6 us
  Pallas kernels  27 us (97%)
  between operations  0.64 us (2%)
    pallas_call x1, Pallas kernels, shards(): pl.pallas_call(functools.partial(kernel, (n_iface, n_dom, hist, base, row...  26.4 us
    pallas_call x1, Pallas kernels, shards(): pl.pallas_call(finish, out_shape=[jax.ShapeDtypeStruct((groups, LANES), F...  0.63 us

profile of v5, /device:TPU:0, one launch (start us, length us, event | category | flops | bytes accessed | tf_op | source)
XLA Modules:
  0.0 27.6 jit_solution(3135864168054083939)
XLA Ops:
  0.6 26.4 %coupling.1 = (f32[32,128]{1,0:T(8,128)S(1)}, f32[32,128]{1,0:T(8,128)S(1)}) custom-call(f32[32,128]{1,0:T(8,128)} %bitcast.7, f32[32,128]{1,0:T(8,128)} %bitcast.8, f32[32,128]{1,0:T(8,128)} %bitcast.9, f32[32,128]{1,0:T(8,128)} %bitcast.10, f32[32,128]{1,0:T(8,128)} %bitcast.11, f32[100,4096]{1,0:T(8,128)} %history_residual.1, f32[100,4096]{1,0:T(8,128)} %history_estimate.1), custom_call_target="tpu_custom_call" | custom-call | tf_op jit(solution)/shard_map/coupling/pallas_call | solution.py:541
  27.0 0.6 %finish.1 = (f32[32,128]{1,0:T(8,128)}, f32[32,128]{1,0:T(8,128)}) custom-call(f32[32,128]{1,0:T(8,128)S(1)} %get-tuple-element.6.a, f32[32,128]{1,0:T(8,128)S(1)} %get-tuple-element.7.b), custom_call_target="tpu_custom_call" | custom-call | tf_op jit(solution)/shard_map/finish/pallas_call | solution.py:587
